TPU v7x, 32 devices: a whole 2x2x4 slice. The times are simulated.
32 devices in a mesh: shard: 8 (over z, x), rep: 4 (over y, core).
Axes of the slice: x: 2, y: 2, z: 4, core: 2. Of those that a mesh axis runs over, the one named last changes fastest.
Arguments:
- lender_block: int32 [96, 8], P(('shard', 'rep')), may hold values from 0 to 255, as said below
- confidence: bfloat16 [96, 8, 256, 256], P(('shard', 'rep')), may hold values from 0 to 80, as said below
- lender_factors: bfloat16 [65536, 128], P('shard'), may hold values from -4 to 4
Outputs:
- borrower_factors: float32 [24576, 128], P(('shard', 'rep'))
- lender_rhs: float32 [65536, 128], P('shard')
Inputs may be any that keep to these rules, and one draw needn't show every extreme that they name: `lender_block`: within one device's 3 borrower blocks, at most 6 of the 3 x 8 entries name blocks of any one owner (block // 32), and on every device some owner is named exactly 6 times. `confidence`: about half the entries are zero; the others are positive.
All inputs are finite; a program needn't handle non-finite values.
Results may differ from a plain program's by a relative error of at most 0.0047.
Values may be sent and summed in bfloat16 or wider, within the bound.
A program may use at most 128 MiB of HBM per device.

v0:
```python
import jax
import jax.numpy as jnp
from jax import lax
from jax.sharding import PartitionSpec as P

CG_STEPS = 3
HIGH = lax.Precision.HIGHEST


def apply_system(direction, confidence, fetched, gram):
    low = direction.astype(jnp.bfloat16)
    scores = jnp.einsum("btr,bklr->bktl", low, fetched, preferred_element_type=jnp.float32)
    weighted = (confidence.astype(jnp.float32) * scores).astype(jnp.bfloat16)
    back = jnp.einsum("bktl,bklr->btr", weighted, fetched, preferred_element_type=jnp.float32)
    width = direction.shape[-1]
    global_part = jnp.dot(
        direction.reshape(-1, width), gram, precision=HIGH, preferred_element_type=jnp.float32
    )
    return global_part.reshape(direction.shape) + 0.1 * direction + back


WIRE = jnp.float16
TOP = 14.0
EXTRA = 16


def encode(value):
    largest = jnp.maximum(jnp.max(jnp.abs(value)), 1e-30)
    level = jnp.ceil(jnp.log2(largest))
    return ((value * jnp.exp2(TOP - level)).astype(WIRE), level)


def with_level(chunks, level):
    head = jnp.broadcast_to(level.astype(WIRE), (chunks.shape[0], EXTRA, chunks.shape[2]))
    return jnp.concatenate([chunks, head], axis=1)


def decode(packed, rows):
    level = packed[:, rows : rows + 1, :1].astype(jnp.float32)
    return packed[:, :rows].astype(jnp.float32) * jnp.exp2(level - TOP)


def per_device(lender_block, confidence, lender_factors):
    shards = lax.axis_size("shard")
    blocks, lists = lender_block.shape
    tile = confidence.shape[2]
    rank = lender_factors.shape[1]
    owned = lender_factors.shape[0] // tile
    entries = blocks * lists
    slots = (2 * entries + shards - 1) // shards
    reps = lax.axis_size("rep")
    me = lax.axis_index("shard")
    part = tile // reps
    local_gram = lax.dot_general(
        lender_factors, lender_factors, (((0,), (0,)), ((), ())), preferred_element_type=jnp.float32
    )
    flat = lender_block.reshape(entries)
    listed = lax.all_gather(flat, ("shard", "rep"), axis=0, tiled=False)
    mine = (listed // owned == me).astype(jnp.int32)
    place = jnp.cumsum(mine, axis=1) - 1
    slot_ids = jnp.arange(slots, dtype=jnp.int32)
    hit = (place[:, :, None] == slot_ids) & (mine[:, :, None] == 1)
    within = listed - owned * me
    named = jnp.sum(jnp.where(hit, within[:, :, None] + 1, 0), axis=1) - 1
    owner = flat // owned
    member = (owner[:, None] == jnp.arange(shards, dtype=jnp.int32)[None, :]).astype(jnp.int32)
    position = jnp.sum(jnp.cumsum(member, axis=0) * member, axis=1) - 1
    slot_index = owner * slots + position
    table = lender_factors.reshape(owned, tile, rank)
    incoming = lax.dynamic_index_in_dim(
        named.reshape(shards, reps, slots), lax.axis_index("rep"), axis=1, keepdims=False
    )
    wanted = table[jnp.maximum(incoming, 0)]
    wanted, local_gram = lax.optimization_barrier((wanted, local_gram))
    gram = lax.psum(local_gram, "shard")
    replies = lax.all_to_all(wanted, "shard", split_axis=0, concat_axis=0, tiled=True)
    fetched = replies.reshape(shards * slots, tile, rank)[slot_index].reshape(
        blocks, lists, tile, rank
    )
    rhs = jnp.einsum("bktl,bklr->btr", confidence, fetched, preferred_element_type=jnp.float32)
    solution = jnp.zeros_like(rhs)
    resid = rhs
    direction = rhs
    norm_now = jnp.sum(resid * resid, axis=2, keepdims=True)
    for count in range(CG_STEPS):
        image = apply_system(direction, confidence, fetched, gram)
        alpha = norm_now / (jnp.sum(direction * image, axis=2, keepdims=True) + 1e-06)
        solution = solution + alpha * direction
        resid = resid - alpha * image
        norm_next = jnp.sum(resid * resid, axis=2, keepdims=True)
        direction = resid + norm_next / (norm_now + 1e-06) * direction
        norm_now = norm_next
    solved = solution.astype(jnp.bfloat16)
    partial_rhs = jnp.einsum(
        "bktl,btr->bklr", confidence, solved, preferred_element_type=jnp.float32
    )
    coded, level = encode(partial_rhs)
    every = jnp.arange(shards * slots, dtype=jnp.int32)
    source = jnp.argmax(slot_index[None, :] == every[:, None], axis=1).astype(jnp.int32)
    quarter = jnp.arange(reps, dtype=jnp.int32)
    pick = source.reshape(shards, 1, slots) * reps + quarter[None, :, None]
    chunks = coded.reshape(entries * reps, part, rank)[pick.reshape(-1)]
    chunks = chunks.reshape(shards * reps, slots * part, rank)
    outgoing = with_level(chunks, level)
    returned = lax.all_to_all(outgoing, ("shard", "rep"), split_axis=0, concat_axis=0, tiled=True)
    back = decode(returned, slots * part)
    selector = (named.reshape(-1)[None, :] == jnp.arange(owned, dtype=jnp.int32)[:, None]).astype(
        jnp.float32
    )
    owner_sum = jnp.dot(
        selector,
        back.reshape(shards * reps * slots, part * rank),
        precision=HIGH,
        preferred_element_type=jnp.float32,
    )
    coded, level = encode(owner_sum.reshape(owned * part, rank))
    shared = lax.all_gather(with_level(coded[None], level)[0], "rep", axis=0, tiled=False)
    lenders_all = owned * tile * shards
    total = decode(shared, owned * part) / lenders_all
    lender_rhs = total.reshape(reps, owned, part, rank).transpose(1, 0, 2, 3)
    lender_rhs = lender_rhs.reshape(owned * tile, rank)
    return (solution.reshape(blocks * tile, rank), lender_rhs)


def solution(mesh):
    in_specs = (P(("shard", "rep"), None), P(("shard", "rep"), None, None, None), P("shard", None))
    out_specs = (P(("shard", "rep"), None), P("shard", None))
    return jax.shard_map(
        per_device, mesh=mesh, in_specs=in_specs, out_specs=out_specs, check_vma=False
    )
```

profile of v0, /device:TPU:0, one launch (start us, length us, event | category | flops | bytes accessed | tf_op | source)
XLA Modules:
  0.0 330.6 jit_solution(16797563167929177055)
XLA Ops:
  7.2 0.9 reshape.352
  8.1 43.3 %all-gather = s32[32,1,24]{2,1,0:T(1,128)S(1)} all-gather(s32[1,1,24]{2,1,0:T(1,128)S(1)} %reshape.352), channel_id=1, replica_groups=mesh['shard'=8,'rep'=4] {'shard','rep'}, dimensions={0}, use_global_device_ids=true | all-gather | bytes 3168 | tf_op jit(solution)/shard_map/all_gather | solution.py:58
  52.3 1.4 fusion.62
  53.7 2.7 gather_fusion
  56.4 4.6 %all-to-all-start = ((bf16[8,6,256,128]{3,2,1,0:T(8,128)(2,1)}), bf16[8,6,256,128]{3,2,1,0:T(8,128)(2,1)}, u32[]{:S(2)}, u32[]{:S(2)}) async-start(bf16[8,6,256,128]{3,2,1,0:T(8,128)(2,1)} %bitcast.109), calls=%async_computation | async-start | bytes 6291456 | tf_op jit(solution)/shard_map/all_to_all | solution.py:76
  63.0 4.7 %copy.162 = bf16[3,8,256,256]{2,3,1,0:T(8,128)(2,1)} copy(bf16[3,8,256,256]{3,2,1,0:T(8,128)(2,1)} %param.4) | data formatting | bytes 6291456 | tf_op args[1]
  67.7 66.2 %all-to-all-done = bf16[8,6,256,128]{3,2,1,0:T(8,128)(2,1)} async-done(((bf16[8,6,256,128]{3,2,1,0:T(8,128)(2,1)}), bf16[8,6,256,128]{3,2,1,0:T(8,128)(2,1)}, u32[]{:S(2)}, u32[]{:S(2)}) %all-to-all-start) | async-done | bytes 3145760 | tf_op jit(solution)/shard_map/all_to_all | solution.py:76
  133.9 3.8 %gather_fusion.1 = bf16[24,256,128]{2,1,0:T(8,128)(2,1)} fusion(bf16[48,256,128]{2,1,0:T(8,128)(2,1)} %bitcast.3, s32[1024]{0:T(1024)S(1)} %pad_clamp_fusion.1), kind=kCustom, calls=%fused_computation.1 | custom fusion | bytes 3145824 | tf_op jit(solution)/shard_map/gather | solution.py:77
  137.7 3.5 %convolution_bitcast_fusion = f32[3,256,128]{1,2,0:T(8,128)S(1)} fusion(bf16[3,8,256,128]{3,2,1,0:T(8,128)(2,1)} %bitcast.111, bf16[3,8,256,256]{3,2,1,0:T(8,128)(2,1)} %param.4), kind=kOutput, calls=%fused_computation.26 | convolution fusion | flops 402653184 | bytes 5111808 | tf_op jit(solution)/shard_map/bktl,bklr->btr/dot_general | solution.py:80
  141.3 4.3 %fusion.16 = f32[3,256,128]{1,2,0:T(8,128)S(1)} fusion(bf16[3,8,256,128]{3,2,1,0:T(8,128)(2,1)} %bitcast.112, bf16[3,8,256,256]{2,3,1,0:T(8,128)(2,1)} %copy.162, f32[3,256,128]{1,2,0:T(8,128)S(1)} %convolution_bitcast_fusion), kind=kOutput, calls=%fused_computation.20 | convolution fusion | flops 810123264 | bytes 5505024 | tf_op jit(solution)/shard_map/bktl,bklr->btr/dot_general | solution.py:14
  145.6 20.3 %all-reduce.4.cloned.1.call-done = f32[128,128]{1,0:T(8,128)} async-done(((f32[128,128]{1,0:T(8,128)}), f32[128,128]{1,0:T(8,128)}) %all-reduce.4.cloned.1.call-update) | async-done | bytes 65552 | tf_op jit(solution)/shard_map/psum | solution.py:75
  165.9 1.4 multiply_reduce_fusion.3
  167.5 5.1 %fusion.19 = f32[3,256,128]{1,2,0:T(8,128)} fusion(bf16[3,8,256,128]{3,2,1,0:T(8,128)(2,1)} %bitcast.113, bf16[3,8,256,256]{2,3,1,0:T(8,128)(2,1)} %copy.162, f32[3,256,128]{1,2,0:T(8,128)S(1)} %multiply_add_fusion.2), kind=kOutput, calls=%fused_computation.21 | convolution fusion | flops 810123264 | bytes 5505024 | tf_op jit(solution)/shard_map/bktl,bklr->btr/dot_general | solution.py:14
  172.6 1.6 multiply_reduce_fusion.1
  175.1 5.2 %fusion.22 = f32[3,256,128]{1,2,0:T(8,128)} fusion(bf16[3,8,256,128]{3,2,1,0:T(8,128)(2,1)} %bitcast.114, bf16[3,8,256,256]{2,3,1,0:T(8,128)(2,1)} %copy.162, f32[3,256,128]{1,2,0:T(8,128)} %multiply_add_fusion.1), kind=kOutput, calls=%fused_computation.22 | convolution fusion | flops 810123264 | bytes 5505024 | tf_op jit(solution)/shard_map/bktl,bklr->btr/dot_general | solution.py:14
  180.2 1.6 fusion.29
  181.8 1.1 multiply_add_fusion
  182.9 4.7 %abs_reduce_fusion = (f32[]{:T(128)}, f32[3,128,8,256]{3,1,2,0:T(8,128)}) fusion(bf16[3,8,256,256]{3,2,1,0:T(8,128)(2,1)} %param.4, f32[3,256,128]{1,2,0:T(8,128)S(1)} %multiply_add_fusion), kind=kOutput, calls=%fused_computation.15 | convolution fusion | flops 404324352 | bytes 6684676 | tf_op jit(solution)/shard_map/bktl,btr->bklr/dot_general | solution.py:94
  188.4 3.5 %fusion.15 = f16[3,8,256,128]{2,3,1,0:T(8,128)(2,1)} fusion(f32[3,128,8,256]{3,1,2,0:T(8,128)} %get-tuple-element.18, f32[]{:T(128)S(6)} %exp2.28), kind=kLoop, calls=%fused_computation.19 | loop fusion | flops 1572864 | bytes 4718596 | tf_op jit(solution)/shard_map/convert_element_type | solution.py:30
  191.9 3.0 copy.178
  194.9 4.8 %gather_fusion.2 = f16[192,64,128]{2,1,0:T(8,128)(2,1)} fusion(f16[96,64,128]{2,1,0:T(8,128)(2,1)} %bitcast.108, s32[1024]{0:T(1024)S(1)} %pad_clamp_fusion), kind=kCustom, calls=%fused_computation.2 | custom fusion | bytes 6292224 | tf_op jit(solution)/shard_map/gather | solution.py:102
  199.7 4.2 %concatenate.6 = f16[32,400,128]{2,1,0:T(8,128)(2,1)} pad(f16[32,384,128]{2,1,0:T(8,128)(2,1)} %bitcast.110, f16[]{:T(256)S(6)} %convert_element_type.82), padding=0_0x0_16x0_0 | pad | bytes 6422530 | tf_op jit(solution)/shard_map/concatenate | solution.py:35
  203.9 4.8 %all-to-all-start.1 = ((f16[32,400,128]{2,1,0:T(8,128)(2,1)}), f16[32,400,128]{2,1,0:T(8,128)(2,1)}, u32[]{:S(2)}, u32[]{:S(2)}) async-start(f16[32,400,128]{2,1,0:T(8,128)(2,1)} %concatenate.6), calls=%async_computation.1 | async-start | bytes 6553600 | tf_op jit(solution)/shard_map/all_to_all | solution.py:105
  208.9 0.9 copy.176
  209.9 73.1 %all-to-all-done.1 = f16[32,400,128]{2,1,0:T(8,128)(2,1)} async-done(((f16[32,400,128]{2,1,0:T(8,128)(2,1)}), f16[32,400,128]{2,1,0:T(8,128)(2,1)}, u32[]{:S(2)}, u32[]{:S(2)}) %all-to-all-start.1) | async-done | bytes 3276832 | tf_op jit(solution)/shard_map/all_to_all | solution.py:105
  284.0 5.3 %convert_multiply_fusion.3 = f32[32,384,128]{2,1,0:T(8,128)} fusion(f16[32,400,128]{2,1,0:T(8,128)(2,1)} %all-to-all-done.1, f32[32]{0:T(128)S(1)} %exponential_bitcast_fusion), kind=kLoop, calls=%fused_computation.9 | loop fusion | flops 3145728 | bytes 9437312 | tf_op jit(solution)/shard_map/mul | solution.py:40
  289.3 7.2 %reshape.323 = f32[192,8192]{1,0:T(8,128)} reshape(f32[32,384,128]{2,1,0:T(8,128)} %convert_multiply_fusion.3) | data formatting | bytes 12582912 | tf_op jit(solution)/shard_map/reshape | solution.py:112
  296.4 5.9 %abs_reduce_fusion.1 = (f32[]{:T(128)}, f32[32,8192]{1,0:T(8,128)S(1)}) fusion(f32[192,8192]{1,0:T(8,128)} %reshape.323, s32[192]{0:T(256)S(1)} %sub.66), kind=kOutput, calls=%fused_computation.33 | convolution fusion | flops 604510208 | bytes 7340804 | tf_op jit(solution)/shard_map/dot_general | solution.py:110
  303.1 0.9 multiply_convert_fusion.1
  304.0 1.3 convert_element_type.86
  305.5 15.4 %all-gather.2 = f16[4,2064,128]{2,1,0:T(8,128)(2,1)S(1)} all-gather(f16[1,2064,128]{2,1,0:T(8,128)(2,1)S(1)} %concatenate.7), channel_id=1, replica_groups=mesh['shard'=8,'rep'=4] {'rep'}, dimensions={0}, use_global_device_ids=true | all-gather | bytes 2641920 | tf_op jit(solution)/shard_map/all_gather | solution.py:117
  321.5 2.3 copy.180
  (57 shorter events, 5.8 us)
Async XLA Ops:
  7.2 45.1 %copy-start = (bf16[8192,128]{1,0:T(8,128)(2,1)S(1)}, bf16[8192,128]{1,0:T(8,128)(2,1)}, u32[]{:S(2)}) copy-start(bf16[8192,128]{1,0:T(8,128)(2,1)} %param.5) | copy-start | bytes 6291460
  56.4 5.3 %copy-start.3 = (s32[3,8]{1,0:T(4,128)S(1)}, s32[3,8]{1,0:T(4,128)}, u32[]{:S(2)}) copy-start(s32[3,8]{1,0:T(4,128)} %param.3) | copy-start | bytes 292
  56.4 77.5 %all-to-all-start = ((bf16[8,6,256,128]{3,2,1,0:T(8,128)(2,1)}), bf16[8,6,256,128]{3,2,1,0:T(8,128)(2,1)}, u32[]{:S(2)}, u32[]{:S(2)}) async-start(bf16[8,6,256,128]{3,2,1,0:T(8,128)(2,1)} %bitcast.109), calls=%async_computation | async-start | bytes 6291456 | tf_op jit(solution)/shard_map/all_to_all | solution.py:76
  60.9 104.9 %all-reduce.4.cloned.1.call-start = ((), (), s32[]{:S(2)}) async-start(), calls=%async_computation.2 | async-start | bytes 131072 | tf_op jit(solution)/shard_map/psum | solution.py:75
  167.5 5.1 %copy-start.2 = (f32[128,128]{1,0:T(8,128)S(1)}, f32[128,128]{1,0:T(8,128)}, u32[]{:S(2)}) copy-start(f32[128,128]{1,0:T(8,128)} %all-reduce.4.cloned.1.call-done) | copy-start | bytes 196612
  175.1 5.2 %copy-start.1 = (f32[3,256,128]{1,2,0:T(8,128)S(1)}, f32[3,256,128]{1,2,0:T(8,128)}, u32[]{:S(2)}) copy-start(f32[3,256,128]{1,2,0:T(8,128)} %multiply_add_fusion.1) | copy-start | bytes 1179652
  203.9 79.1 %all-to-all-start.1 = ((f16[32,400,128]{2,1,0:T(8,128)(2,1)}), f16[32,400,128]{2,1,0:T(8,128)(2,1)}, u32[]{:S(2)}, u32[]{:S(2)}) async-start(f16[32,400,128]{2,1,0:T(8,128)(2,1)} %concatenate.6), calls=%async_computation.1 | async-start | bytes 6553600 | tf_op jit(solution)/shard_map/all_to_all | solution.py:105
Sparse Core Ops, SparseCore 0:
  65.7 100.0 all-reduce.3
where the time goes:
time: 332 us; the launch traced here: 331 us
  waiting for transfers between devices  160 us (48%)
  blocking collectives  58.7 us (18%)
  local copies, waits for them, and re-layouts  38.1 us (11%)
  matrix products  34.7 us (10%)
  between operations  15.7 us (5%)
  other arithmetic  13.7 us (4%)
  starting transfers between devices  9.45 us (3%)
    all_to_all x1, waiting for transfers between devices, per_device(): lax.all_to_all(outgoing, ('shard', 'rep'), split_axis=0, concat_axis=0, t...  73.1 us
    all_to_all x1, waiting for transfers between devices, per_device(): lax.all_to_all(wanted, 'shard', split_axis=0, concat_axis=0, tiled=True)  66.2 us
    all_gather x1, blocking collectives, per_device(): listed = lax.all_gather(flat, ('shard', 'rep'), axis=0, tiled=False)  43.3 us
    psum x1, waiting for transfers between devices, per_device(): gram = lax.psum(local_gram, 'shard')  20.3 us
    all_gather x1, blocking collectives, per_device(): lax.all_gather(with_level(coded[None], level)[0], 'rep', axis=0, tiled=Fa...  15.4 us
    dot_general x3, matrix products, apply_system(): jnp.einsum('bktl,bklr->btr', weighted, fetched, preferred_element_type=jn...  14.5 us
    reshape x1, local copies, waits for them, and re-layouts, per_device(): back.reshape(shards * reps * slots, part * rank)  7.15 us
  transfers between devices with their start and end apart: 3, of which 3 were waited for; matrix products, arithmetic and copies ran while one was open for 6% of the time, Pallas kernels for 0%

commit v1 on v0

--- a/solution.py
+++ b/solution.py
@@ -5,6 +5,10 @@
 
 CG_STEPS = 3
 HIGH = lax.Precision.HIGHEST
+
+
+def tell_orders_up(frame):
+    return jnp.sum(jax.lax.all_gather(frame, "shard"), axis=0)
 
 
 def apply_system(direction, confidence, fetched, gram):
@@ -72,7 +76,7 @@
     )
     wanted = table[jnp.maximum(incoming, 0)]
     wanted, local_gram = lax.optimization_barrier((wanted, local_gram))
-    gram = lax.psum(local_gram, "shard")
+    gram = tell_orders_up(local_gram)
     replies = lax.all_to_all(wanted, "shard", split_axis=0, concat_axis=0, tiled=True)
     fetched = replies.reshape(shards * slots, tile, rank)[slot_index].reshape(
         blocks, lists, tile, rank

time: 332 us -> 315 us (0.949)
  waiting for transfers between devices: 160 us -> 73.3 us
  blocking collectives: 58.7 us -> 145 us
  between operations: 15.7 us -> 2.37 us
    all_gather x0 -> x1, blocking collectives: none -> 86.5 us  [tell_orders_up(): return jnp.sum(jax.lax.all_gather(frame, 'shard'), axis=0)]
    all_to_all x1, waiting for transfers between devices: 66.2 us -> 0.01 us  [per_device(): lax.all_to_all(wanted, 'shard', split_axis=0, concat_axis=0, tiled=True)]
    psum x1 -> x0, waiting for transfers between devices: 20.3 us -> none  [per_device(): gram = lax.psum(local_gram, 'shard')]
  transfers between devices with their start and end apart: 3 -> 2, of which waited for: 3 -> 1; matrix products, arithmetic and copies ran while one was open for 6% -> 2% of each run, Pallas kernels for 0% -> 0%
where the time goes in v1:
time: 315 us; the launch traced here: 314 us
  blocking collectives  145 us (46%)
  waiting for transfers between devices  73.3 us (23%)
  local copies, waits for them, and re-layouts  38 us (12%)
  matrix products  33.2 us (11%)
  other arithmetic  13.8 us (4%)
  starting transfers between devices  8.33 us (3%)
    all_gather x1, blocking collectives, tell_orders_up(): return jnp.sum(jax.lax.all_gather(frame, 'shard'), axis=0)  86.5 us
    all_to_all x1, waiting for transfers between devices, per_device(): lax.all_to_all(outgoing, ('shard', 'rep'), split_axis=0, concat_axis=0, t...  73.3 us
    all_gather x1, blocking collectives, per_device(): listed = lax.all_gather(flat, ('shard', 'rep'), axis=0, tiled=False)  43.3 us
    all_gather x1, blocking collectives, per_device(): lax.all_gather(with_level(coded[None], level)[0], 'rep', axis=0, tiled=Fa...  15.3 us
    dot_general x3, matrix products, apply_system(): jnp.einsum('bktl,bklr->btr', weighted, fetched, preferred_element_type=jn...  14.5 us
    reshape x1, local copies, waits for them, and re-layouts, per_device(): back.reshape(shards * reps * slots, part * rank)  7.15 us
  transfers between devices with their start and end apart: 2, of which 1 were waited for; matrix products, arithmetic and copies ran while one was open for 2% of the time, Pallas kernels for 0%

profile of v1, /device:TPU:0, one launch (start us, length us, event | category | flops | bytes accessed | tf_op | source)
XLA Modules:
  0.0 314.1 jit_solution(11973449196371604702)
XLA Ops:
  0.6 0.9 reshape.353
  1.6 43.3 %all-gather.1 = s32[32,1,24]{2,1,0:T(1,128)S(1)} all-gather(s32[1,1,24]{2,1,0:T(1,128)S(1)} %reshape.353), channel_id=1, replica_groups=mesh['shard'=8,'rep'=4] {'shard','rep'}, dimensions={0}, use_global_device_ids=true | all-gather | bytes 3168 | tf_op jit(solution)/shard_map/all_gather | solution.py:62
  45.7 0.7 fusion.62
  46.5 2.7 gather_fusion
  49.2 4.6 %all-to-all-start = ((bf16[8,6,256,128]{3,2,1,0:T(8,128)(2,1)}), bf16[8,6,256,128]{3,2,1,0:T(8,128)(2,1)}, u32[]{:S(2)}, u32[]{:S(2)}) async-start(bf16[8,6,256,128]{3,2,1,0:T(8,128)(2,1)} %bitcast.110), calls=%async_computation | async-start | bytes 6291456 | tf_op jit(solution)/shard_map/all_to_all | solution.py:80
  55.1 4.7 %copy.165 = bf16[3,8,256,256]{2,3,1,0:T(8,128)(2,1)} copy(bf16[3,8,256,256]{3,2,1,0:T(8,128)(2,1)} %param.4) | data formatting | bytes 6291456 | tf_op args[1]
  59.8 86.5 %all-gather = f32[1024,128]{1,0:T(8,128)S(1)} all-gather(f32[128,128]{1,0:T(8,128)S(1)} %fusion.62), channel_id=2, replica_groups=mesh['shard'=8,'rep'=4] {'shard'}, dimensions={0}, use_global_device_ids=true | all-gather | bytes 589824 | tf_op jit(solution)/shard_map/all_gather | solution.py:11
  146.5 3.8 %gather_fusion.1 = bf16[24,256,128]{2,1,0:T(8,128)(2,1)} fusion(bf16[48,256,128]{2,1,0:T(8,128)(2,1)} %bitcast.3, s32[1024]{0:T(1024)S(1)} %pad_clamp_fusion.1), kind=kCustom, calls=%fused_computation.1 | custom fusion | bytes 3145824 | tf_op jit(solution)/shard_map/gather | solution.py:81
  150.3 3.5 %convolution_bitcast_fusion = f32[3,256,128]{1,2,0:T(8,128)S(1)} fusion(bf16[3,8,256,128]{3,2,1,0:T(8,128)(2,1)} %bitcast.112, bf16[3,8,256,256]{3,2,1,0:T(8,128)(2,1)} %param.4), kind=kOutput, calls=%fused_computation.26 | convolution fusion | flops 402653184 | bytes 5111808 | tf_op jit(solution)/shard_map/bktl,bklr->btr/dot_general | solution.py:84
  153.8 4.3 %fusion.16 = f32[3,256,128]{1,2,0:T(8,128)S(1)} fusion(bf16[3,8,256,128]{3,2,1,0:T(8,128)(2,1)} %bitcast.113, bf16[3,8,256,256]{2,3,1,0:T(8,128)(2,1)} %copy.165, f32[3,256,128]{1,2,0:T(8,128)S(1)} %convolution_bitcast_fusion), kind=kOutput, calls=%fused_computation.20 | convolution fusion | flops 810123264 | bytes 5505024 | tf_op jit(solution)/shard_map/bktl,bklr->btr/dot_general | solution.py:18
  158.9 5.0 %fusion.19 = f32[3,256,128]{1,2,0:T(8,128)} fusion(bf16[3,8,256,128]{3,2,1,0:T(8,128)(2,1)} %bitcast.114, bf16[3,8,256,256]{2,3,1,0:T(8,128)(2,1)} %copy.165, f32[3,256,128]{1,2,0:T(8,128)S(1)} %multiply_add_fusion.2), kind=kOutput, calls=%fused_computation.21 | convolution fusion | flops 810123264 | bytes 5505024 | tf_op jit(solution)/shard_map/bktl,bklr->btr/dot_general | solution.py:18
  163.9 1.6 multiply_reduce_fusion.1
  165.6 0.8 multiply_add_fusion.1
  166.4 5.2 %fusion.22 = f32[3,256,128]{1,2,0:T(8,128)} fusion(bf16[3,8,256,128]{3,2,1,0:T(8,128)(2,1)} %bitcast.115, bf16[3,8,256,256]{2,3,1,0:T(8,128)(2,1)} %copy.165, f32[3,256,128]{1,2,0:T(8,128)} %multiply_add_fusion.1), kind=kOutput, calls=%fused_computation.22 | convolution fusion | flops 810123264 | bytes 5505024 | tf_op jit(solution)/shard_map/bktl,bklr->btr/dot_general | solution.py:18
  171.6 1.6 fusion.29
  173.2 1.1 multiply_add_fusion
  174.3 4.7 %abs_reduce_fusion = (f32[]{:T(128)}, f32[3,128,8,256]{3,1,2,0:T(8,128)}) fusion(bf16[3,8,256,256]{3,2,1,0:T(8,128)(2,1)} %param.4, f32[3,256,128]{1,2,0:T(8,128)S(1)} %multiply_add_fusion), kind=kOutput, calls=%fused_computation.15 | convolution fusion | flops 404324352 | bytes 6684676 | tf_op jit(solution)/shard_map/bktl,btr->bklr/dot_general | solution.py:98
  179.8 3.5 %fusion.15 = f16[3,8,256,128]{2,3,1,0:T(8,128)(2,1)} fusion(f32[3,128,8,256]{3,1,2,0:T(8,128)} %get-tuple-element.18, f32[]{:T(128)S(6)} %exp2.28), kind=kLoop, calls=%fused_computation.19 | loop fusion | flops 1572864 | bytes 4718596 | tf_op jit(solution)/shard_map/convert_element_type | solution.py:34
  183.3 3.0 copy.181
  186.2 4.8 %gather_fusion.2 = f16[192,64,128]{2,1,0:T(8,128)(2,1)} fusion(f16[96,64,128]{2,1,0:T(8,128)(2,1)} %bitcast.109, s32[1024]{0:T(1024)S(1)} %pad_clamp_fusion), kind=kCustom, calls=%fused_computation.2 | custom fusion | bytes 6292224 | tf_op jit(solution)/shard_map/gather | solution.py:106
  191.0 4.2 %concatenate.6 = f16[32,400,128]{2,1,0:T(8,128)(2,1)} pad(f16[32,384,128]{2,1,0:T(8,128)(2,1)} %bitcast.111, f16[]{:T(256)S(6)} %convert_element_type.82), padding=0_0x0_16x0_0 | pad | bytes 6422530 | tf_op jit(solution)/shard_map/concatenate | solution.py:39
  195.3 3.8 %all-to-all-start.1 = ((f16[32,400,128]{2,1,0:T(8,128)(2,1)}), f16[32,400,128]{2,1,0:T(8,128)(2,1)}, u32[]{:S(2)}, u32[]{:S(2)}) async-start(f16[32,400,128]{2,1,0:T(8,128)(2,1)} %concatenate.6), calls=%async_computation.1 | async-start | bytes 6553600 | tf_op jit(solution)/shard_map/all_to_all | solution.py:109
  199.2 0.9 copy.179
  200.2 73.3 %all-to-all-done.1 = f16[32,400,128]{2,1,0:T(8,128)(2,1)} async-done(((f16[32,400,128]{2,1,0:T(8,128)(2,1)}), f16[32,400,128]{2,1,0:T(8,128)(2,1)}, u32[]{:S(2)}, u32[]{:S(2)}) %all-to-all-start.1) | async-done | bytes 3276832 | tf_op jit(solution)/shard_map/all_to_all | solution.py:109
  273.4 0.9 slice.23
  274.4 5.3 %convert_multiply_fusion.3 = f32[32,384,128]{2,1,0:T(8,128)} fusion(f16[32,400,128]{2,1,0:T(8,128)(2,1)} %all-to-all-done.1, f32[32]{0:T(128)S(1)} %exponential_bitcast_fusion), kind=kLoop, calls=%fused_computation.9 | loop fusion | flops 3145728 | bytes 9437312 | tf_op jit(solution)/shard_map/mul | solution.py:44
  279.7 7.2 %reshape.323 = f32[192,8192]{1,0:T(8,128)} reshape(f32[32,384,128]{2,1,0:T(8,128)} %convert_multiply_fusion.3) | data formatting | bytes 12582912 | tf_op jit(solution)/shard_map/reshape | solution.py:116
  286.9 5.9 %abs_reduce_fusion.1 = (f32[]{:T(128)}, f32[32,8192]{1,0:T(8,128)S(1)}) fusion(f32[192,8192]{1,0:T(8,128)} %reshape.323, s32[192]{0:T(256)S(1)} %sub.66), kind=kOutput, calls=%fused_computation.33 | convolution fusion | flops 604510208 | bytes 7340804 | tf_op jit(solution)/shard_map/dot_general | solution.py:114
  293.5 0.9 multiply_convert_fusion.1
  294.4 1.3 convert_element_type.86
  295.9 15.3 %all-gather.3 = f16[4,2064,128]{2,1,0:T(8,128)(2,1)S(1)} all-gather(f16[1,2064,128]{2,1,0:T(8,128)(2,1)S(1)} %concatenate.7), channel_id=1, replica_groups=mesh['shard'=8,'rep'=4] {'rep'}, dimensions={0}, use_global_device_ids=true | all-gather | bytes 2641920 | tf_op jit(solution)/shard_map/all_gather | solution.py:121
  311.7 2.3 copy.183
  (54 shorter events, 4.1 us)
Async XLA Ops:
  0.6 45.1 %copy-start = (bf16[8192,128]{1,0:T(8,128)(2,1)S(1)}, bf16[8192,128]{1,0:T(8,128)(2,1)}, u32[]{:S(2)}) copy-start(bf16[8192,128]{1,0:T(8,128)(2,1)} %param.5) | copy-start | bytes 6291460
  49.2 4.6 %copy-start.2 = (s32[3,8]{1,0:T(4,128)S(1)}, s32[3,8]{1,0:T(4,128)}, u32[]{:S(2)}) copy-start(s32[3,8]{1,0:T(4,128)} %param.3) | copy-start | bytes 292
  49.2 97.2 %all-to-all-start = ((bf16[8,6,256,128]{3,2,1,0:T(8,128)(2,1)}), bf16[8,6,256,128]{3,2,1,0:T(8,128)(2,1)}, u32[]{:S(2)}, u32[]{:S(2)}) async-start(bf16[8,6,256,128]{3,2,1,0:T(8,128)(2,1)} %bitcast.110), calls=%async_computation | async-start | bytes 6291456 | tf_op jit(solution)/shard_map/all_to_all | solution.py:80
  166.4 5.2 %copy-start.1 = (f32[3,256,128]{1,2,0:T(8,128)S(1)}, f32[3,256,128]{1,2,0:T(8,128)}, u32[]{:S(2)}) copy-start(f32[3,256,128]{1,2,0:T(8,128)} %multiply_add_fusion.1) | copy-start | bytes 1179652
  195.3 78.1 %all-to-all-start.1 = ((f16[32,400,128]{2,1,0:T(8,128)(2,1)}), f16[32,400,128]{2,1,0:T(8,128)(2,1)}, u32[]{:S(2)}, u32[]{:S(2)}) async-start(f16[32,400,128]{2,1,0:T(8,128)(2,1)} %concatenate.6), calls=%async_computation.1 | async-start | bytes 6553600 | tf_op jit(solution)/shard_map/all_to_all | solution.py:109
